TPU v7x, 32 devices: a whole 2x2x4 slice. The times are simulated.
32 devices in a mesh: groups: 2 (over x), holders: 16 (over z, y, core).
Axes of the slice: x: 2, y: 2, z: 4, core: 2. Of those that a mesh axis runs over, the one named last changes fastest.
Arguments:
- q_nope: bfloat16 [2, 256, 128], P(None, ('groups', 'holders')), parts along dimension 1, may hold values from -6 to 6
- q_rope: bfloat16 [2, 256, 64], P(None, ('groups', 'holders')), parts along dimension 1, may hold values from -30 to 30
- w_uk: bfloat16 [2, 16, 128, 512], replicated, may hold values from -0.5 to 0.5
- w_uv: bfloat16 [2, 16, 512, 128], replicated, may hold values from -0.25 to 0.25
- new_latent: bfloat16 [2, 16, 576], P(None, 'groups'), parts along dimension 1, may hold values from -33 to 33
- shallow_cache: bfloat16 [1, 256, 512, 576], P(None, ('groups', 'holders')), parts along dimension 1, may hold values from -30 to 30
- slot_positions: int32 [1, 256, 512], P(None, ('groups', 'holders')), parts along dimension 1, may hold values from 0 to 131071
- slab_map: int32 [1, 256], P(None, 'groups'), parts along dimension 1, may hold values from 0 to 127, each once within a row
- deep_cache: bfloat16 [1, 16, 256, 576], P(None, 'groups'), parts along dimension 1, may hold values from -30 to 30
- deep_positions: int32 [1, 16, 256], P(None, 'groups'), parts along dimension 1, may hold values from 0 to 131071
- lengths: int32 [16], P('groups'), parts along dimension 0, may hold values from 1 to 131072
Outputs:
- attended: bfloat16 [2, 256, 128], P(None, ('groups', 'holders')), parts along dimension 1
There are 2 independent parts, one for each index of `groups`. A program takes and returns all parts, laid end to end along the dimension named above; an argument that names none is the same for every part. Nothing has to cross between parts.
Inputs may be any that keep to these rules, and one draw needn't show every extreme that they name: Each row of slab_map names every slot once; entry b * 16 + s is the slot of request b's slab s.
All inputs are finite; a program needn't handle non-finite values.
Results may differ from a plain program's by a relative error of at most 0.0065.
Values may be sent and summed in bfloat16 or wider, within the bound.
A program may use at most 64 MiB of HBM per device.

v0:
```python
import jax
import jax.numpy as jnp
from jax import lax
from jax.sharding import PartitionSpec as P

HEADS = 16
LATENT = 512
BATCH = 8
SLABS_REQ = 16


score_scale = 192.0 ** (-0.5)
neg_fill = -1e30


def block_partials(query_rows, keys, live):
    score = (
        jnp.einsum("nhc,ntc->nht", query_rows, keys, preferred_element_type=jnp.float32)
        * score_scale
    )
    block_max = jnp.max(jnp.where(live, score, neg_fill), axis=-1)
    weight = jnp.where(
        live, jnp.exp(jnp.where(live, score - block_max[..., None], 0.0)), 0.0
    ).astype(jnp.bfloat16)
    block_sum = jnp.sum(weight.astype(jnp.float32), axis=-1)
    block_out = jnp.einsum(
        "nht,ntc->nhc", weight, keys[..., :LATENT], preferred_element_type=jnp.float32
    )
    return (block_max, block_sum, block_out)


def shards(
    q_nope,
    q_rope,
    w_uk,
    w_uv,
    new_latent,
    shallow_cache,
    slot_positions,
    slab_map,
    deep_cache,
    deep_positions,
    lengths,
):
    rows_dev = q_nope.shape[1]
    holder_count = lax.axis_size("holders")
    start = lax.axis_index("holders") * rows_dev
    row_ids = start + jnp.arange(rows_dev, dtype=jnp.int32)
    head_ids = row_ids % HEADS
    row_req = row_ids // HEADS
    shallow_count = shallow_cache.shape[0]
    slot_dev = shallow_cache.shape[1]
    all_slots = slab_map.shape[1]
    per_req = max(1, rows_dev // HEADS)
    rows_req = rows_dev // per_req
    first_req = start // HEADS

    def own_query(layer):
        own_lat = jnp.einsum(
            "rd,rdc->rc", q_nope[layer], w_uk[layer][head_ids], preferred_element_type=jnp.float32
        ).astype(jnp.bfloat16)
        return jnp.concatenate([own_lat, q_rope[layer]], axis=-1)

    results = []
    for layer in range(q_nope.shape[0]):
        if layer < shallow_count:
            query_own = own_query(layer)
            query_all = lax.all_gather(query_own, "holders", axis=0, tiled=True).reshape(
                BATCH, HEADS, -1
            )
            slot_ids = lax.axis_index("holders") * slot_dev + jnp.arange(slot_dev, dtype=jnp.int32)
            owner_req = jnp.arange(all_slots, dtype=jnp.int32) // SLABS_REQ
            matches = slab_map[layer][None, :] == slot_ids[:, None]
            slot_req = jnp.sum(jnp.where(matches, owner_req[None, :], 0), axis=1)
            live = (slot_positions[layer] < lengths[slot_req][:, None])[:, None, :]
            slot_max, slot_sum, slot_out = block_partials(
                query_all[slot_req], shallow_cache[layer], live
            )
            chosen = slot_req[None, :] == jnp.arange(BATCH, dtype=jnp.int32)[:, None]
            dense_max = jnp.max(jnp.where(chosen[:, :, None], slot_max[None], neg_fill), axis=1)
            factor = jnp.where(
                chosen[:, :, None],
                jnp.exp(jnp.minimum(slot_max[None] - dense_max[:, None, :], 0.0)),
                0.0,
            )
            dense_sum = jnp.einsum("bjh,jh->bh", factor, slot_sum, precision=lax.Precision.HIGHEST)
            dense_out = jnp.einsum(
                "bjh,jhc->bhc", factor, slot_out, precision=lax.Precision.HIGHEST
            )
            flat_max = dense_max.reshape(-1)
            flat_sum = dense_sum.reshape(-1)
            flat_out = dense_out.reshape(BATCH * HEADS, -1)
            piece_max, piece_sum, piece_out = (
                lax.all_to_all(
                    flat_max.reshape(holder_count, rows_dev),
                    "holders",
                    split_axis=0,
                    concat_axis=0,
                    tiled=True,
                ),
                lax.all_to_all(
                    flat_sum.reshape(holder_count, rows_dev),
                    "holders",
                    split_axis=0,
                    concat_axis=0,
                    tiled=True,
                ),
                lax.all_to_all(
                    flat_out.reshape(holder_count, rows_dev, -1),
                    "holders",
                    split_axis=0,
                    concat_axis=0,
                    tiled=True,
                ),
            )
            own_max = jnp.max(piece_max, axis=0)
            source_factor = jnp.exp(piece_max - own_max[None])
            own_sum = jnp.sum(piece_sum * source_factor, axis=0)
            own_out = jnp.sum(piece_out * source_factor[..., None], axis=0)
        else:
            query_own = own_query(layer)
            deep_layer = layer - shallow_count
            deep_keys = lax.dynamic_slice_in_dim(deep_cache[deep_layer], first_req, per_req, 0)
            deep_where = lax.dynamic_slice_in_dim(deep_positions[deep_layer], first_req, per_req, 0)
            limits = lax.dynamic_slice_in_dim(lengths, first_req, per_req, 0)
            live = (deep_where < limits[:, None])[:, None, :]
            deep_max, deep_sum, deep_out = block_partials(
                query_own.reshape(per_req, rows_req, -1), deep_keys, live
            )
            own_max = deep_max.reshape(-1)
            own_sum = deep_sum.reshape(-1)
            own_out = deep_out.reshape(rows_dev, -1)
        newlat = new_latent[layer][row_req].astype(jnp.float32)
        own_score = jnp.sum(query_own.astype(jnp.float32) * newlat, axis=-1) * score_scale
        top = jnp.maximum(own_score, own_max)
        own_factor = jnp.exp(own_score - top)
        far_factor = jnp.exp(own_max - top)
        total = own_factor + own_sum * far_factor
        mixed = (
            (own_factor[:, None] * newlat[:, :LATENT] + own_out * far_factor[:, None])
            / total[:, None]
        ).astype(jnp.bfloat16)
        attended = jnp.einsum(
            "rc,rcv->rv", mixed, w_uv[layer][head_ids], preferred_element_type=jnp.float32
        )
        results.append(attended.astype(jnp.bfloat16))
    return jnp.stack(results, axis=0)


def solution(mesh):
    return jax.shard_map(
        shards,
        mesh=mesh,
        in_specs=(
            P(None, ("groups", "holders"), None),
            P(None, ("groups", "holders"), None),
            P(),
            P(),
            P(None, "groups", None),
            P(None, ("groups", "holders"), None, None),
            P(None, ("groups", "holders"), None),
            P(None, "groups"),
            P(None, "groups", None, None),
            P(None, "groups", None),
            P("groups"),
        ),
        out_specs=P(None, ("groups", "holders"), None),
        check_vma=False,
    )
```

profile of v0, /device:TPU:0, one launch (start us, length us, event | category | flops | bytes accessed | tf_op | source)
XLA Modules:
  0.0 97.8 jit_solution(10515259585690447637)
XLA Ops:
  0.0 1.0 %select_reduce_fusion.3 = s32[8]{0:T(128)S(1)} fusion(s32[128]{0:T(128)S(1)} %and_select_fusion, s32[128]{0:T(128)} %bitcast.104, s32[8]{0:T(128)S(1)} %iota_add_fusion), kind=kLoop, calls=%fused_computation.75 | loop fusion | flops 3064 | bytes 1088 | tf_op jit(solution)/shard_map/reduce_sum | solution.py:74
  1.1 0.7 slice_bitcast_fusion.11
  1.8 0.7 slice_bitcast_fusion.10
  2.5 4.7 %slice_bitcast_fusion.3 = (bf16[16,128,512]{2,1,0:T(8,128)(2,1)}, bf16[16,128,512]{2,1,0:T(8,128)(2,1)}) fusion(bf16[2,16,128,512]{3,2,1,0:T(8,128)(2,1)} %param.13), kind=kLoop, calls=%fused_computation.15 | loop fusion | bytes 8388608 | tf_op jit(solution)/shard_map/squeeze | solution.py:60
  7.1 2.2 %gather_fusion = bf16[8,128,512]{2,1,0:T(8,128)(2,1)S(1)} fusion(bf16[16,128,512]{2,1,0:T(8,128)(2,1)} %get-tuple-element.13, s32[1024]{0:T(1024)S(1)} %pad_clamp_fusion.2), kind=kCustom, calls=%fused_computation | custom fusion | bytes 2097184 | tf_op jit(solution)/shard_map/gather | solution.py:60
  9.6 23.6 %all_gather.3 = bf16[128,576]{1,0:T(8,128)(2,1)S(1)} all-gather(bf16[8,576]{1,0:T(8,128)(2,1)S(1)} %pad_maximum_fusion), channel_id=1, replica_groups=mesh['groups'=2,'holders'=16] {'holders'}, dimensions={0}, use_global_device_ids=true | all-gather | bytes 156672 | tf_op jit(solution)/shard_map/all_gather | solution.py:68
  33.2 0.6 gather_fusion.2
  33.8 0.6 gather_fusion.3
  34.5 3.2 %select_reduce_fusion = (f32[8,16]{1,0:T(8,128)S(1)}, f32[8,16,512]{2,1,0:T(8,128)S(1)}) fusion(pred[8,512]{1,0:T(8,128)(4,1)S(1)} %bitcast_compare_fusion, bf16[8,16,576]{2,1,0:T(8,128)(2,1)S(1)} %gather_fusion.3, bf16[1,8,512,576]{2,3,1,0:T(8,128)(2,1)} %param.16), kind=kOutput, calls=%fused_computation.30 | convolution fusion | flops 75693952 | bytes 5132800 | tf_op jit(solution)/shard_map/nhc,ntc->nht/dot_general | solution.py:18
  38.0 0.7 all_to_all.19
  38.6 3.5 %all-to-all-start = ((f32[16,1,8]{2,1,0:T(1,128)}), f32[16,1,8]{2,1,0:T(1,128)S(1)}, u32[]{:S(2)}, u32[]{:S(2)}) async-start(f32[16,1,8]{2,1,0:T(1,128)} %bitcast.17), calls=%async_computation | async-start | bytes 16384 | tf_op jit(solution)/shard_map/all_to_all | solution.py:94
  42.2 7.7 %copy.34 = bf16[1,8,512,576]{3,2,1,0:T(8,128)(2,1)} copy(bf16[1,8,512,576]{2,3,1,0:T(8,128)(2,1)} %param.16) | data formatting | bytes 9437184 | tf_op args[5]
  49.9 0.6 dynamic_slice.12
  50.5 0.6 gather_fusion.6
  51.1 0.7 dynamic-slice_bitcast_fusion
  52.1 2.2 %gather_fusion.5 = bf16[8,128,512]{2,1,0:T(8,128)(2,1)S(1)} fusion(bf16[16,128,512]{2,1,0:T(8,128)(2,1)} %get-tuple-element.14, s32[1024]{0:T(1024)S(1)} %pad_clamp_fusion.2), kind=kCustom, calls=%fused_computation.5 | custom fusion | bytes 2097184 | tf_op jit(solution)/shard_map/gather | solution.py:60
  54.5 1.4 %compare_reduce_fusion = pred[256]{0:T(512)(128)(4,1)S(1)} fusion(s32[1,8,256]{2,1,0:T(8,128)} %param.20, s32[]{:T(128)S(6)} %select_n.127, s32[]{:T(128)} %bitcast.35), kind=kLoop, calls=%fused_computation.76 | loop fusion | flops 256 | bytes 1288 | tf_op jit(solution)/shard_map/lt | solution.py:126
  56.0 0.3 select_reduce_fusion.2
  56.3 4.7 %slice_bitcast_fusion.2 = (bf16[16,512,128]{2,1,0:T(8,128)(2,1)}, bf16[16,512,128]{2,1,0:T(8,128)(2,1)}) fusion(bf16[2,16,512,128]{3,2,1,0:T(8,128)(2,1)} %param.14), kind=kLoop, calls=%fused_computation.14 | loop fusion | bytes 8388608 | tf_op jit(solution)/shard_map/squeeze | solution.py:144
  61.0 2.3 %gather_fusion.7 = bf16[8,512,128]{2,1,0:T(8,128)(2,1)S(1)} fusion(bf16[16,512,128]{2,1,0:T(8,128)(2,1)} %get-tuple-element.16, s32[1024]{0:T(1024)S(1)} %pad_clamp_fusion.2), kind=kCustom, calls=%fused_computation.7 | custom fusion | bytes 2097184 | tf_op jit(solution)/shard_map/gather | solution.py:144
  63.4 3.0 %fusion.2 = f32[8,16,512]{2,1,0:T(8,128)S(1)} fusion(bf16[8,512,576]{2,1,0:T(8,128)(2,1)} %bitcast.94, f32[8,16,512]{2,1,0:T(8,128)} %copy-done.2, f32[8,16]{1,0:T(8,128)S(1)} %get-tuple-element.25, pred[8,512]{1,0:T(8,128)(4,1)S(1)} %bitcast_compare_fusion), kind=kOutput, calls=%fused_computation.10 | convolution fusion | flops 67371008 | bytes 4723200 | tf_op jit(solution)/shard_map/nht,ntc->nhc/dot_general | solution.py:26
  66.4 1.2 %convolution_bitcast_fusion = f32[8,16,512]{2,0,1:T(8,128)} fusion(f32[8,16,512]{2,1,0:T(8,128)S(1)} %fusion.2, f32[8,16]{0,1:T(8,128)S(1)} %select_reduce_fusion.1, f32[8,16]{0,1:T(8,128)S(1)} %copy.36, pred[8,8]{1,0:T(8,128)(4,1)S(1)} %iota_compare_fusion), kind=kOutput, calls=%fused_computation.17 | convolution fusion | flops 6294528 | bytes 525376 | tf_op jit(solution)/shard_map/bjh,jhc->bhc/dot_general | solution.py:87
  68.5 0.7 all_to_all.23
  69.2 6.0 %all-to-all-start.2 = ((f32[16,1,8]{2,1,0:T(1,128)}), f32[16,1,8]{2,1,0:T(1,128)S(1)}, u32[]{:S(2)}, u32[]{:S(2)}) async-start(f32[16,1,8]{2,1,0:T(1,128)} %bitcast.22), calls=%async_computation.2 | async-start | bytes 16384 | tf_op jit(solution)/shard_map/all_to_all | solution.py:101
  75.2 0.6 gather_fusion.1
  75.7 1.8 %copy.40 = f32[8,16,512]{2,1,0:T(8,128)} copy(f32[8,16,512]{2,0,1:T(8,128)} %convolution_bitcast_fusion) | data formatting | bytes 524288 | tf_op jit(solution)/shard_map/bjh,jhc->bhc/transpose | solution.py:87
  77.5 4.0 %all-to-all-done.2 = f32[16,1,8]{2,1,0:T(1,128)S(1)} async-done(((f32[16,1,8]{2,1,0:T(1,128)}), f32[16,1,8]{2,1,0:T(1,128)S(1)}, u32[]{:S(2)}, u32[]{:S(2)}) %all-to-all-start.2) | async-done | bytes 544 | tf_op jit(solution)/shard_map/all_to_all | solution.py:101
  81.6 4.2 %all-to-all-start.1 = ((f32[16,8,512]{2,1,0:T(8,128)}), f32[16,8,512]{2,1,0:T(8,128)}, u32[]{:S(2)}, u32[]{:S(2)}) async-start(f32[16,8,512]{2,1,0:T(8,128)} %bitcast.19), calls=%async_computation.1 | async-start | bytes 524288 | tf_op jit(solution)/shard_map/all_to_all | solution.py:108
  85.9 2.3 %gather_fusion.4 = bf16[8,512,128]{2,1,0:T(8,128)(2,1)S(1)} fusion(bf16[16,512,128]{2,1,0:T(8,128)(2,1)} %get-tuple-element.15, s32[1024]{0:T(1024)S(1)} %pad_clamp_fusion.2), kind=kCustom, calls=%fused_computation.4 | custom fusion | bytes 2097184 | tf_op jit(solution)/shard_map/gather | solution.py:144
  88.7 7.1 %all-to-all-done.1 = f32[16,8,512]{2,1,0:T(8,128)} async-done(((f32[16,8,512]{2,1,0:T(8,128)}), f32[16,8,512]{2,1,0:T(8,128)}, u32[]{:S(2)}, u32[]{:S(2)}) %all-to-all-start.1) | async-done | bytes 262176 | tf_op jit(solution)/shard_map/all_to_all | solution.py:108
  95.8 1.0 %multiply_reduce_fusion = f32[8,512]{1,0:T(8,128)S(1)} fusion(f32[16,8,512]{2,1,0:T(8,128)} %all-to-all-done.1, f32[16,8]{1,0:T(8,128)S(1)} %copy.42), kind=kLoop, calls=%fused_computation.28 | loop fusion | flops 126976 | bytes 279040 | tf_op jit(solution)/shard_map/reduce_sum | solution.py:119
  97.2 0.6 pad_maximum_fusion.3
  (53 shorter events, 3.1 us)
Async XLA Ops:
  0.0 51.0 %copy-start = (bf16[1,8,256,576]{2,3,1,0:T(8,128)(2,1)S(1)}, bf16[1,8,256,576]{2,3,1,0:T(8,128)(2,1)}, u32[]{:S(2)}) copy-start(bf16[1,8,256,576]{2,3,1,0:T(8,128)(2,1)} %param.19) | copy-start | bytes 7077892
  7.1 26.1 %copy-start.1 = (s32[8]{0:T(128)S(1)}, s32[8]{0:T(128)}, u32[]{:S(2)}) copy-start(s32[8]{0:T(128)} %param.21) | copy-start | bytes 100
  7.1 27.3 %copy-start.5 = (s32[1,8,512]{2,1,0:T(8,128)S(1)}, s32[1,8,512]{2,1,0:T(8,128)}, u32[]{:S(2)}) copy-start(s32[1,8,512]{2,1,0:T(8,128)} %param.17) | copy-start | bytes 49156
  37.7 14.1 %copy-start.2 = (f32[8,16,512]{2,1,0:T(8,128)}, f32[8,16,512]{2,1,0:T(8,128)S(1)}, u32[]{:S(2)}) copy-start(f32[8,16,512]{2,1,0:T(8,128)S(1)} %get-tuple-element.26) | copy-start | bytes 786436
  38.6 30.6 %all-to-all-start = ((f32[16,1,8]{2,1,0:T(1,128)}), f32[16,1,8]{2,1,0:T(1,128)S(1)}, u32[]{:S(2)}, u32[]{:S(2)}) async-start(f32[16,1,8]{2,1,0:T(1,128)} %bitcast.17), calls=%async_computation | async-start | bytes 16384 | tf_op jit(solution)/shard_map/all_to_all | solution.py:94
  42.1 8.3 %copy-start.4 = (bf16[2,8,576]{2,1,0:T(8,128)(2,1)S(1)}, bf16[2,8,576]{2,1,0:T(8,128)(2,1)}, u32[]{:S(2)}) copy-start(bf16[2,8,576]{2,1,0:T(8,128)(2,1)} %param.15) | copy-start | bytes 55300
  63.3 4.5 %copy-start.3 = (bf16[1,256,576]{1,2,0:T(8,128)(2,1)S(1)}, bf16[1,256,576]{1,2,0:T(8,128)(2,1)}, u32[]{:S(2)}) copy-start(bf16[1,256,576]{1,2,0:T(8,128)(2,1)} %dynamic-slice_bitcast_fusion) | copy-start | bytes 884740
  69.2 12.4 %all-to-all-start.2 = ((f32[16,1,8]{2,1,0:T(1,128)}), f32[16,1,8]{2,1,0:T(1,128)S(1)}, u32[]{:S(2)}, u32[]{:S(2)}) async-start(f32[16,1,8]{2,1,0:T(1,128)} %bitcast.22), calls=%async_computation.2 | async-start | bytes 16384 | tf_op jit(solution)/shard_map/all_to_all | solution.py:101
  81.6 14.2 %all-to-all-start.1 = ((f32[16,8,512]{2,1,0:T(8,128)}), f32[16,8,512]{2,1,0:T(8,128)}, u32[]{:S(2)}, u32[]{:S(2)}) async-start(f32[16,8,512]{2,1,0:T(8,128)} %bitcast.19), calls=%async_computation.1 | async-start | bytes 524288 | tf_op jit(solution)/shard_map/all_to_all | solution.py:108
where the time goes:
time: 98.6 us; the launch traced here: 97.8 us
  local copies, waits for them, and re-layouts  34.9 us (35%)
  blocking collectives  23.6 us (24%)
  starting transfers between devices  13.6 us (14%)
  waiting for transfers between devices  11.2 us (11%)
  matrix products  8.87 us (9%)
  other arithmetic  5.39 us (5%)
    all_gather x1, blocking collectives, shards(): lax.all_gather(query_own, 'holders', axis=0, tiled=True)  23.6 us
    unnamed x14, local copies, waits for them, and re-layouts  7.8 us
    all_to_all x1, waiting for transfers between devices, shards(): lax.all_to_all(flat_out.reshape(holder_count, rows_dev, -1), 'holders', s...  7.1 us
    all_to_all x1, starting transfers between devices, shards(): lax.all_to_all(flat_sum.reshape(holder_count, rows_dev), 'holders', split...  5.95 us
    squeeze x1, local copies, waits for them, and re-layouts, shards(): w_uv[layer][head_ids]  4.7 us
    gather x2, local copies, waits for them, and re-layouts, shards(): w_uv[layer][head_ids]  4.68 us
    squeeze x1, local copies, waits for them, and re-layouts, own_query(): w_uk[layer][head_ids]  4.66 us
    gather x2, local copies, waits for them, and re-layouts, own_query(): w_uk[layer][head_ids]  4.43 us
  transfers between devices with their start and end apart: 3, of which 2 were waited for; matrix products, arithmetic and copies ran while one was open for 32% of the time, Pallas kernels for 0%

commit v1 on v0

v1 whole, which is shorter than its diff:
```python
import functools

import jax
import jax.numpy as jnp
from jax import lax
from jax.experimental import pallas as pl
from jax.experimental.pallas import tpu as pltpu
from jax.sharding import PartitionSpec as P

HEADS = 16
LATENT = 512
SLABS_REQ = 16

score_scale = 192.0 ** (-0.5)
neg_fill = -1e30

f32 = jnp.float32
bf16 = jnp.bfloat16


def dot(a, b):
    return lax.dot_general(a, b, (((1,), (0,)), ((), ())), preferred_element_type=f32)


def dot_t(a, b):
    return lax.dot_general(a, b, (((1,), (1,)), ((), ())), preferred_element_type=f32)


def iota(shape, dim):
    return lax.broadcasted_iota(jnp.int32, shape, dim)


def lane_sum(mask, values):
    return jnp.sum(jnp.where(mask, values, jnp.zeros_like(values)), axis=1, keepdims=True)


def row_sum(mask, values):
    return jnp.sum(jnp.where(mask, values, jnp.zeros_like(values)), axis=0, keepdims=True)


def one_hot(mask):
    return jnp.where(mask, 1.0, 0.0).astype(bf16)


def kernel(
    n, dims,
    lengths, q_nope, q_rope, w_uk, w_uv, new_latent, cache, positions, slab_map,
    deep_cache, deep_positions,
    out,
    qn_all, qr_all, qn_deep, qr_deep, uk0, uv0, uk1, uv1, newlat, keys, pos, smap,
    dkeys, dpos, qlat, slot_out, proj, outbox, inbox,
    loc_sem, slab_sem, qn_send, qn_recv, qr_send, qr_recv, o_send, o_recv,
):
    rows_dev, slots, batch = dims
    rows = n * rows_dev
    srows = slots * HEADS
    me = lax.axis_index("holders")
    start = me * rows_dev
    head0 = lax.rem(start, HEADS)
    req = lax.div(start, HEADS)
    pad = max(8, rows_dev)
    unroll = n <= 16

    local = [
        (q_nope.at[0], qn_all.at[me]),
        (q_rope.at[0], qr_all.at[me]),
        (q_nope.at[1], qn_deep),
        (q_rope.at[1], qr_deep),
        (w_uk.at[1, pl.ds(head0, rows_dev)], uk1),
        (new_latent, newlat),
        (deep_positions.at[0], dpos),
        (deep_cache.at[0, req], dkeys),
        (w_uv.at[1, pl.ds(head0, rows_dev)], uv1),
        (slab_map, smap),
        (positions.at[0], pos),
        (w_uk.at[0], uk0),
        (w_uv.at[0], uv0),
    ]
    local = [pltpu.make_async_copy(s, d, loc_sem.at[i]) for i, (s, d) in enumerate(local)]
    slab_copies = [
        pltpu.make_async_copy(cache.at[0, j], keys.at[j], slab_sem.at[j]) for j in range(slots)
    ]

    for c in local[:2]:
        c.start()

    barrier = pltpu.get_barrier_semaphore()

    def greet(k, carry):
        peer = lax.rem(me + k, n)
        pl.semaphore_signal(
            barrier, inc=1, device_id={"holders": peer}, device_id_type=pl.DeviceIdType.MESH
        )
        return carry

    lax.fori_loop(1, n, greet, 0, unroll=unroll)
    for c in local[2:12]:
        c.start()
    for c in slab_copies:
        c.start()
    local[12].start()
    local[0].wait()
    local[1].wait()
    pl.semaphore_wait(barrier, n - 1)

    def remote(src, dst, ssem, rsem, k):
        peer = lax.rem(me + k, n)
        return pltpu.make_async_remote_copy(
            src_ref=src, dst_ref=dst, send_sem=ssem.at[k], recv_sem=rsem.at[k],
            device_id={"holders": peer}, device_id_type=pl.DeviceIdType.MESH,
        )

    def q_copies(k):
        return (
            remote(qn_all.at[me], qn_all.at[me], qn_send, qn_recv, k),
            remote(qr_all.at[me], qr_all.at[me], qr_send, qr_recv, k),
        )

    def send_q(k, carry):
        for c in q_copies(k):
            c.start()
        return carry

    lax.fori_loop(1, n, send_q, 0, unroll=unroll)

    def widen(x):
        if x.shape[0] < pad:
            x = jnp.concatenate([x] * (pad // x.shape[0]), axis=0)
        return x

    own_row = lax.rem(iota((pad, 1), 0), rows_dev)

    def per_head(x, head_of):
        acc = None
        for i in range(rows_dev):
            part = dot(x, head_of(i))
            acc = part if acc is None else jnp.where(own_row == i, part, acc)
        return acc

    for c in local[2:9]:
        c.wait()
    pick = iota((batch, newlat.shape[2]), 0) == req
    new1 = row_sum(pick, newlat[1].astype(f32))
    new0 = row_sum(pick, newlat[0].astype(f32))
    qn1 = widen(qn_deep[...].astype(f32)).astype(bf16)
    qr1 = widen(qr_deep[...].astype(f32)).astype(bf16)
    ql1 = per_head(qn1, lambda i: uk1[i]).astype(bf16)
    score = (dot_t(ql1, dkeys[:, :LATENT]) + dot_t(qr1, dkeys[:, LATENT:])) * score_scale
    where1 = row_sum(iota(dpos.shape, 0) == req, dpos[...])
    live = where1 < lengths[req]
    own_max = jnp.max(jnp.where(live, score, neg_fill), axis=1, keepdims=True)
    weight = jnp.where(live, jnp.exp(jnp.where(live, score - own_max, 0.0)), 0.0).astype(bf16)
    own_sum = jnp.sum(weight.astype(f32), axis=1, keepdims=True)
    own_out = dot(weight, dkeys[:, :LATENT])

    def own_scores(ql, qr, new):
        lat = jnp.sum(ql.astype(f32) * new[:, :LATENT], axis=1, keepdims=True)
        rot = jnp.sum(qr.astype(f32) * new[:, LATENT:], axis=1, keepdims=True)
        return (lat + rot) * score_scale

    own_score = own_scores(ql1, qr1, new1)
    top = jnp.maximum(own_score, own_max)
    own_f = jnp.exp(own_score - top)
    far_f = jnp.exp(own_max - top)
    total = own_f + own_sum * far_f
    mixed = ((own_f * new1[:, :LATENT] + own_out * far_f) / total).astype(bf16)
    attended1 = per_head(mixed, lambda i: uv1[i])
    out[1] = attended1[:rows_dev].astype(bf16)

    for c in local[9:12]:
        c.wait()
    r_s = iota((srows, rows), 0)
    c_s = iota((srows, rows), 1)
    found = smap[...] == me * slots + lax.div(iota((srows, smap.shape[1]), 0), HEADS)
    req_col = lane_sum(found, lax.div(iota((srows, smap.shape[1]), 1), SLABS_REQ))
    len_col = jnp.zeros((srows, 1), jnp.int32)
    for b in range(batch):
        len_col = jnp.where(req_col == b, lengths[b], len_col)
    sel_bh = (lax.div(c_s, HEADS) == req_col) & (lax.rem(c_s, HEADS) == lax.rem(r_s, HEADS))
    sel_hb = (lax.rem(c_s, batch) == req_col) & (lax.div(c_s, batch) == lax.rem(r_s, HEADS))
    sel_bh, sel_hb = one_hot(sel_bh), one_hot(sel_hb)
    r_q = iota((rows, rows), 0)
    c_q = iota((rows, rows), 1)
    perm = (lax.rem(r_q, batch) == lax.div(c_q, HEADS)) & (lax.div(r_q, batch) == lax.rem(c_q, HEADS))
    eye = iota((srows, srows), 0) == iota((srows, srows), 1)
    req_row = row_sum(eye, jnp.broadcast_to(req_col, eye.shape))
    r_t = iota((rows, srows), 0)
    c_t = iota((rows, srows), 1)
    back = (lax.div(r_t, batch) == lax.rem(c_t, HEADS)) & (lax.rem(r_t, batch) == req_row)

    def wait_q(k, carry):
        for c in q_copies(k):
            c.wait_recv()
        return carry

    lax.fori_loop(1, n, wait_q, 0, unroll=unroll)
    qn = qn_all[...].astype(f32).reshape(rows, qn_all.shape[2]).astype(bf16)
    qr = qr_all[...].astype(f32).reshape(rows, qr_all.shape[2]).astype(bf16)
    qn_hb = dot(one_hot(perm), qn)
    for h in range(0, HEADS, 2):
        two = [
            dot(qn_hb[g * batch:(g + 1) * batch].astype(bf16), uk0[g]) for g in (h, h + 1)
        ]
        qlat[h * batch:(h + 2) * batch, :] = jnp.concatenate(two, axis=0).astype(bf16)
    q_slot = dot(sel_hb, qlat[...]).astype(bf16)
    r_slot = dot(sel_bh, qr).astype(bf16)

    maxes, sums = [], []
    for j in range(slots):
        at = slice(j * HEADS, (j + 1) * HEADS)
        slab_copies[j].wait()
        score = (
            dot_t(q_slot[at], keys[j, :, :LATENT]) + dot_t(r_slot[at], keys[j, :, LATENT:])
        ) * score_scale
        live = pos[j:j + 1, :] < len_col[at]
        block_max = jnp.max(jnp.where(live, score, neg_fill), axis=1, keepdims=True)
        weight = jnp.where(
            live, jnp.exp(jnp.where(live, score - block_max, 0.0)), 0.0
        ).astype(bf16)
        maxes.append(block_max)
        sums.append(jnp.sum(weight.astype(f32), axis=1, keepdims=True))
        slot_out[at, :] = dot(weight, keys[j, :, :LATENT])
    slot_max = jnp.concatenate(maxes, axis=0)
    slot_sum = jnp.concatenate(sums, axis=0)

    max_row = row_sum(eye, jnp.broadcast_to(slot_max, eye.shape))
    sum_row = row_sum(eye, jnp.broadcast_to(slot_sum, eye.shape))
    dense_max = jnp.max(jnp.where(back, max_row, neg_fill), axis=1, keepdims=True)
    factor_row = jnp.exp(max_row - row_sum(back, jnp.broadcast_to(dense_max, back.shape)))
    dense_sum = lane_sum(back, jnp.broadcast_to(sum_row * factor_row, back.shape))
    factor_col = lane_sum(eye, jnp.broadcast_to(factor_row, eye.shape))
    scaled = (slot_out[...] * factor_col).astype(bf16)
    dense = dot(one_hot(back), scaled)
    local[12].wait()
    for h in range(HEADS):
        part = dot(dense[h * batch:(h + 1) * batch].astype(bf16), uv0[h])
        proj[pl.ds(h, batch, stride=HEADS), :] = part
    outbox[:, :rows_dev, :] = proj[...].reshape(n, rows_dev, proj.shape[1])
    stat_max = row_sum(perm, jnp.broadcast_to(dense_max, perm.shape))
    stat_sum = row_sum(perm, jnp.broadcast_to(dense_sum, perm.shape))
    stats = jnp.concatenate([stat_max, stat_sum], axis=0)
    outbox[:, rows_dev:, :] = jnp.broadcast_to(stats[None], (n,) + stats.shape)
    inbox[me] = outbox[me]

    def o_copy(k):
        return remote(outbox.at[lax.rem(me + k, n)], inbox.at[me], o_send, o_recv, k)

    def send_o(k, carry):
        o_copy(k).start()
        return carry

    lax.fori_loop(1, n, send_o, 0, unroll=unroll)

    qn0 = widen(qn_all[me].astype(f32)).astype(bf16)
    qr0 = widen(qr_all[me].astype(f32)).astype(bf16)
    ql0 = per_head(qn0, lambda i: uk0[head0 + i]).astype(bf16)
    own_score = own_scores(ql0, qr0, new0)
    new_in = jnp.broadcast_to(new0[:, :LATENT], (pad, LATENT)).astype(bf16)
    new_out = per_head(new_in, lambda i: uv0[head0 + i])

    def wait_sent(k, carry):
        for c in q_copies(k):
            c.wait_send()
        return carry

    lax.fori_loop(1, n, wait_sent, 0, unroll=unroll)

    def wait_o(k, carry):
        o_copy(k).wait_recv()
        return carry

    lax.fori_loop(1, n, wait_o, 0, unroll=unroll)
    got_max = inbox[:, rows_dev, :]
    got_sum = inbox[:, rows_dev + 1, :]
    far_max = jnp.max(got_max, axis=0, keepdims=True)
    got_f = jnp.exp(got_max - far_max)
    far_sum = jnp.sum(got_sum * got_f, axis=0, keepdims=True)
    mine = iota((rows_dev, rows), 1) == start + iota((rows_dev, rows), 0)

    def own_rows(x):
        return lane_sum(mine, jnp.broadcast_to(x, mine.shape))

    acc = jnp.zeros((rows_dev, proj.shape[1]), f32)
    for s in range(n):
        acc = acc + own_rows(got_f[s:s + 1]) * inbox[s, :rows_dev, :]
    far_max = own_rows(far_max)
    far_sum = own_rows(far_sum)
    own_score = own_score[:rows_dev]
    top = jnp.maximum(own_score, far_max)
    own_f = jnp.exp(own_score - top)
    far_f = jnp.exp(far_max - top)
    total = own_f + far_sum * far_f
    out[0] = ((own_f * new_out[:rows_dev] + acc * far_f) / total).astype(bf16)

    def wait_o_sent(k, carry):
        o_copy(k).wait_send()
        return carry

    lax.fori_loop(1, n, wait_o_sent, 0, unroll=unroll)


def shards(
    q_nope, q_rope, w_uk, w_uv, new_latent, shallow_cache, slot_positions, slab_map,
    deep_cache, deep_positions, lengths,
):
    n = lax.axis_size("holders")
    rows_dev, nope = q_nope.shape[1:]
    rope = q_rope.shape[2]
    slots, slab, width = shallow_cache.shape[1:]
    batch = new_latent.shape[1]
    value = w_uv.shape[3]
    deep_tok = deep_cache.shape[2]
    dma = pltpu.SemaphoreType.DMA
    any_spec = pl.BlockSpec(memory_space=pl.ANY)
    return pl.pallas_call(
        functools.partial(kernel, n, (rows_dev, slots, batch)),
        out_shape=jax.ShapeDtypeStruct((q_nope.shape[0], rows_dev, value), bf16),
        in_specs=[pl.BlockSpec(memory_space=pltpu.SMEM)] + [any_spec] * 10,
        out_specs=pl.BlockSpec(memory_space=pltpu.VMEM),
        scratch_shapes=[
            pltpu.VMEM((n, rows_dev, nope), bf16),
            pltpu.VMEM((n, rows_dev, rope), bf16),
            pltpu.VMEM((rows_dev, nope), bf16),
            pltpu.VMEM((rows_dev, rope), bf16),
            pltpu.VMEM(w_uk.shape[1:], bf16),
            pltpu.VMEM(w_uv.shape[1:], bf16),
            pltpu.VMEM((rows_dev,) + w_uk.shape[2:], bf16),
            pltpu.VMEM((rows_dev,) + w_uv.shape[2:], bf16),
            pltpu.VMEM(new_latent.shape, bf16),
            pltpu.VMEM((slots, slab, width), bf16),
            pltpu.VMEM((slots, slab), jnp.int32),
            pltpu.VMEM(slab_map.shape, jnp.int32),
            pltpu.VMEM((deep_tok, width), bf16),
            pltpu.VMEM((batch, deep_tok), jnp.int32),
            pltpu.VMEM((n * rows_dev, LATENT), bf16),
            pltpu.VMEM((slots * HEADS, LATENT), f32),
            pltpu.VMEM((n * rows_dev, value), f32),
            pltpu.VMEM((n, rows_dev + 2, value), f32),
            pltpu.VMEM((n, rows_dev + 2, value), f32),
            dma((13,)),
            dma((slots,)),
            dma((n,)),
            dma((n,)),
            dma((n,)),
            dma((n,)),
            dma((n,)),
            dma((n,)),
        ],
        compiler_params=pltpu.CompilerParams(
            collective_id=0, has_side_effects=True, vmem_limit_bytes=60 * 1024 * 1024
        ),
    )(
        lengths, q_nope, q_rope, w_uk, w_uv, new_latent, shallow_cache, slot_positions,
        slab_map, deep_cache, deep_positions,
    )


def solution(mesh):
    return jax.shard_map(
        shards,
        mesh=mesh,
        in_specs=(
            P(None, ("groups", "holders"), None),
            P(None, ("groups", "holders"), None),
            P(),
            P(),
            P(None, "groups", None),
            P(None, ("groups", "holders"), None, None),
            P(None, ("groups", "holders"), None),
            P(None, "groups"),
            P(None, "groups", None, None),
            P(None, "groups", None),
            P("groups"),
        ),
        out_specs=P(None, ("groups", "holders"), None),
        check_vma=False,
    )
```

time: 98.6 us -> 36.2 us (0.37)
  blocking collectives: 23.6 us -> 0 us
  Pallas kernels: 0 us -> 22.5 us
  local copies, waits for them, and re-layouts: 34.9 us -> 13.3 us
  starting transfers between devices: 13.6 us -> 0 us
  waiting for transfers between devices: 11.2 us -> 0 us
  matrix products: 8.87 us -> 0 us
  other arithmetic: 5.39 us -> 0 us
    all_gather x1 -> x0, blocking collectives: 23.6 us -> none  [shards(): lax.all_gather(query_own, 'holders', axis=0, tiled=True)]
    pallas_call x0 -> x1, Pallas kernels: none -> 22.5 us  [shards(): pl.pallas_call(functools.partial(kernel, n, (rows_dev, slots, batch)), ou...]
    all_to_all x3 -> x0, starting transfers between devices: 13.6 us -> none  [the longest x1 5.95 us: shards(): lax.all_to_all(flat_sum.reshape(holder_count, rows_dev), 'holders', split...]
    gather x8 -> x0, local copies, waits for them, and re-layouts: 11.5 us -> none  [the longest x2 4.68 us: shards(): w_uv[layer][head_ids]]
    all_to_all x3 -> x0, waiting for transfers between devices: 11.2 us -> none  [the longest x1 7.1 us: shards(): lax.all_to_all(flat_out.reshape(holder_count, rows_dev, -1), 'holders', s...]
    squeeze x5 -> x0, local copies, waits for them, and re-layouts: 10.8 us -> none  [the longest x1 4.7 us: shards(): w_uv[layer][head_ids]]
    dot_general x9 -> x0, matrix products: 8.87 us -> none  [the longest x2 3.45 us: block_partials(): jnp.einsum('nhc,ntc->nht', query_rows, keys, preferred_element_type=jnp.f...]
    unnamed x14 -> x3, local copies, waits for them, and re-layouts: 7.8 us -> 13.3 us
  transfers between devices with their start and end apart: 3 -> 0, of which waited for: 2 -> 0; matrix products, arithmetic and copies ran while one was open for 32% -> 0% of each run, Pallas kernels for 0% -> 0%
where the time goes in v1:
time: 36.2 us; the launch traced here: 35.9 us
  Pallas kernels  22.5 us (62%)
  local copies, waits for them, and re-layouts  13.3 us (37%)
    pallas_call x1, Pallas kernels, shards(): pl.pallas_call(functools.partial(kernel, n, (rows_dev, slots, batch)), ou...  22.5 us
    unnamed x3, local copies, waits for them, and re-layouts  13.3 us

profile of v1, /device:TPU:0, one launch (start us, length us, event | category | flops | bytes accessed | tf_op | source)
XLA Modules:
  0.0 35.9 jit_solution(6778274687310929228)
XLA Ops:
  0.0 4.3 %copy.13.deep_cache = bf16[1,8,256,576]{3,2,1,0:T(8,128)(2,1)} copy(bf16[1,8,256,576]{2,3,1,0:T(8,128)(2,1)} %param.19) | data formatting | bytes 4718592 | tf_op args[8]
  4.3 7.7 %copy.12.cache = bf16[1,8,512,576]{3,2,1,0:T(8,128)(2,1)} copy(bf16[1,8,512,576]{2,3,1,0:T(8,128)(2,1)} %param.16) | data formatting | bytes 9437184 | tf_op args[5]
  12.0 22.5 %shard_map.109 = bf16[2,8,128]{2,1,0:T(8,128)(2,1)} custom-call(s32[8]{0:T(128)} %lengths.1, bf16[2,8,128]{2,1,0:T(8,128)(2,1)} %q_nope.1, bf16[2,8,64]{2,1,0:T(8,128)(2,1)} %q_rope.1, bf16[2,16,128,512]{3,2,1,0:T(8,128)(2,1)} %w_uk.1, bf16[2,16,512,128]{3,2,1,0:T(8,128)(2,1)} %w_uv.1, bf16[2,8,576]{2,1,0:T(8,128)(2,1)} %new_latent.1, ...), custom_call_target="tpu_custom_call" | custom-call | tf_op jit(solution)/shard_map/pallas_call | solution.py:315
  34.6 1.3 %copy.15 = bf16[2,8,128]{2,1,0:T(8,128)(2,1)} copy(bf16[2,8,128]{2,1,0:T(8,128)(2,1)} %shard_map.109) | data formatting | bytes 8192

commit v2 on v1

--- a/solution.py
+++ b/solution.py
@@ -145,13 +145,13 @@
     qn1 = widen(qn_deep[...].astype(f32)).astype(bf16)
     qr1 = widen(qr_deep[...].astype(f32)).astype(bf16)
     ql1 = per_head(qn1, lambda i: uk1[i]).astype(bf16)
-    score = (dot_t(ql1, dkeys[:, :LATENT]) + dot_t(qr1, dkeys[:, LATENT:])) * score_scale
+    score = (dot(ql1, dkeys[:LATENT]) + dot(qr1, dkeys[LATENT:])) * score_scale
     where1 = row_sum(iota(dpos.shape, 0) == req, dpos[...])
     live = where1 < lengths[req]
     own_max = jnp.max(jnp.where(live, score, neg_fill), axis=1, keepdims=True)
     weight = jnp.where(live, jnp.exp(jnp.where(live, score - own_max, 0.0)), 0.0).astype(bf16)
     own_sum = jnp.sum(weight.astype(f32), axis=1, keepdims=True)
-    own_out = dot(weight, dkeys[:, :LATENT])
+    own_out = dot_t(weight, dkeys[:LATENT])
 
     def own_scores(ql, qr, new):
         lat = jnp.sum(ql.astype(f32) * new[:, :LATENT], axis=1, keepdims=True)
@@ -210,7 +210,7 @@
         at = slice(j * HEADS, (j + 1) * HEADS)
         slab_copies[j].wait()
         score = (
-            dot_t(q_slot[at], keys[j, :, :LATENT]) + dot_t(r_slot[at], keys[j, :, LATENT:])
+            dot(q_slot[at], keys[j, :LATENT]) + dot(r_slot[at], keys[j, LATENT:])
         ) * score_scale
         live = pos[j:j + 1, :] < len_col[at]
         block_max = jnp.max(jnp.where(live, score, neg_fill), axis=1, keepdims=True)
@@ -219,7 +219,7 @@
         ).astype(bf16)
         maxes.append(block_max)
         sums.append(jnp.sum(weight.astype(f32), axis=1, keepdims=True))
-        slot_out[at, :] = dot(weight, keys[j, :, :LATENT])
+        slot_out[at, :] = dot_t(weight, keys[j, :LATENT])
     slot_max = jnp.concatenate(maxes, axis=0)
     slot_sum = jnp.concatenate(sums, axis=0)
 
@@ -327,10 +327,10 @@
             pltpu.VMEM((rows_dev,) + w_uk.shape[2:], bf16),
             pltpu.VMEM((rows_dev,) + w_uv.shape[2:], bf16),
             pltpu.VMEM(new_latent.shape, bf16),
-            pltpu.VMEM((slots, slab, width), bf16),
+            pltpu.VMEM((slots, width, slab), bf16),
             pltpu.VMEM((slots, slab), jnp.int32),
             pltpu.VMEM(slab_map.shape, jnp.int32),
-            pltpu.VMEM((deep_tok, width), bf16),
+            pltpu.VMEM((width, deep_tok), bf16),
             pltpu.VMEM((batch, deep_tok), jnp.int32),
             pltpu.VMEM((n * rows_dev, LATENT), bf16),
             pltpu.VMEM((slots * HEADS, LATENT), f32),
@@ -350,8 +350,8 @@
             collective_id=0, has_side_effects=True, vmem_limit_bytes=60 * 1024 * 1024
         ),
     )(
-        lengths, q_nope, q_rope, w_uk, w_uv, new_latent, shallow_cache, slot_positions,
-        slab_map, deep_cache, deep_positions,
+        lengths, q_nope, q_rope, w_uk, w_uv, new_latent, jnp.swapaxes(shallow_cache, 2, 3),
+        slot_positions, slab_map, jnp.swapaxes(deep_cache, 2, 3), deep_positions,
     )
 
 

time: 36.2 us -> 23.5 us (0.65)
  local copies, waits for them, and re-layouts: 13.3 us -> 1.28 us
  Pallas kernels: 22.5 us -> 22 us
    unnamed x3 -> x1, local copies, waits for them, and re-layouts: 13.3 us -> 1.28 us
    pallas_call x1, Pallas kernels: 22.5 us -> 22 us  [shards(): pl.pallas_call(functools.partial(kernel, n, (rows_dev, slots, batch)), ou...]
where the time goes in v2:
time: 23.5 us; the launch traced here: 23.3 us
  Pallas kernels  22 us (94%)
  local copies, waits for them, and re-layouts  1.28 us (5%)
    pallas_call x1, Pallas kernels, shards(): pl.pallas_call(functools.partial(kernel, n, (rows_dev, slots, batch)), ou...  22 us
    unnamed x1, local copies, waits for them, and re-layouts  1.28 us

profile of v2, /device:TPU:0, one launch (start us, length us, event | category | flops | bytes accessed | tf_op | source)
XLA Modules:
  0.0 23.3 jit_solution(10950330004951833544)
XLA Ops:
  0.0 22.0 %shard_map.109 = bf16[2,8,128]{2,1,0:T(8,128)(2,1)} custom-call(s32[8]{0:T(128)} %lengths.1, bf16[2,8,128]{2,1,0:T(8,128)(2,1)} %q_nope.1, bf16[2,8,64]{2,1,0:T(8,128)(2,1)} %q_rope.1, bf16[2,16,128,512]{3,2,1,0:T(8,128)(2,1)} %w_uk.1, bf16[2,16,512,128]{3,2,1,0:T(8,128)(2,1)} %w_uv.1, bf16[2,8,576]{2,1,0:T(8,128)(2,1)} %new_latent.1, ...), custom_call_target="tpu_custom_call" | custom-call | tf_op jit(solution)/shard_map/pallas_call | solution.py:315
  22.0 1.3 %copy.13 = bf16[2,8,128]{2,1,0:T(8,128)(2,1)} copy(bf16[2,8,128]{2,1,0:T(8,128)(2,1)} %shard_map.109) | data formatting | bytes 8192

commit v3 on v2

--- a/solution.py
+++ b/solution.py
@@ -48,7 +48,7 @@
     deep_cache, deep_positions,
     out,
     qn_all, qr_all, qn_deep, qr_deep, uk0, uv0, uk1, uv1, newlat, keys, pos, smap,
-    dkeys, dpos, qlat, slot_out, proj, outbox, inbox,
+    dkeys, dpos, qlat, score, dead, proj, outbox, inbox,
     loc_sem, slab_sem, qn_send, qn_recv, qr_send, qr_recv, o_send, o_recv,
 ):
     rows_dev, slots, batch = dims
@@ -60,6 +60,7 @@
     req = lax.div(start, HEADS)
     pad = max(8, rows_dev)
     unroll = n <= 16
+    lanes = qlat.shape[2]
 
     local = [
         (q_nope.at[0], qn_all.at[me]),
@@ -145,11 +146,11 @@
     qn1 = widen(qn_deep[...].astype(f32)).astype(bf16)
     qr1 = widen(qr_deep[...].astype(f32)).astype(bf16)
     ql1 = per_head(qn1, lambda i: uk1[i]).astype(bf16)
-    score = (dot(ql1, dkeys[:LATENT]) + dot(qr1, dkeys[LATENT:])) * score_scale
+    score1 = (dot(ql1, dkeys[:LATENT]) + dot(qr1, dkeys[LATENT:])) * score_scale
     where1 = row_sum(iota(dpos.shape, 0) == req, dpos[...])
     live = where1 < lengths[req]
-    own_max = jnp.max(jnp.where(live, score, neg_fill), axis=1, keepdims=True)
-    weight = jnp.where(live, jnp.exp(jnp.where(live, score - own_max, 0.0)), 0.0).astype(bf16)
+    own_max = jnp.max(jnp.where(live, score1, neg_fill), axis=1, keepdims=True)
+    weight = jnp.where(live, jnp.exp(jnp.where(live, score1 - own_max, 0.0)), 0.0).astype(bf16)
     own_sum = jnp.sum(weight.astype(f32), axis=1, keepdims=True)
     own_out = dot_t(weight, dkeys[:LATENT])
 
@@ -171,22 +172,32 @@
         c.wait()
     r_s = iota((srows, rows), 0)
     c_s = iota((srows, rows), 1)
-    found = smap[...] == me * slots + lax.div(iota((srows, smap.shape[1]), 0), HEADS)
-    req_col = lane_sum(found, lax.div(iota((srows, smap.shape[1]), 1), SLABS_REQ))
+    own_slots = me * slots
+    entry = lax.div(iota((srows, smap.shape[1]), 1), SLABS_REQ)
+    map_row = iota((srows, smap.shape[1]), 0)
+    by_slot = lane_sum(smap[...] == own_slots + lax.div(map_row, HEADS), entry)
+    by_head = lane_sum(smap[...] == own_slots + lax.rem(map_row, slots), entry)
     len_col = jnp.zeros((srows, 1), jnp.int32)
     for b in range(batch):
-        len_col = jnp.where(req_col == b, lengths[b], len_col)
-    sel_bh = (lax.div(c_s, HEADS) == req_col) & (lax.rem(c_s, HEADS) == lax.rem(r_s, HEADS))
-    sel_hb = (lax.rem(c_s, batch) == req_col) & (lax.div(c_s, batch) == lax.rem(r_s, HEADS))
-    sel_bh, sel_hb = one_hot(sel_bh), one_hot(sel_hb)
-    r_q = iota((rows, rows), 0)
-    c_q = iota((rows, rows), 1)
-    perm = (lax.rem(r_q, batch) == lax.div(c_q, HEADS)) & (lax.div(r_q, batch) == lax.rem(c_q, HEADS))
+        len_col = jnp.where(by_slot == b, lengths[b], len_col)
+    c_req, c_head = lax.div(c_s, HEADS), lax.rem(c_s, HEADS)
+    sel = (c_req == by_slot) & (c_head == lax.rem(r_s, HEADS))
+    sel_hot = one_hot(sel)
+    sel_head = one_hot((c_req == by_head) & (c_head == lax.div(r_s, slots)))
     eye = iota((srows, srows), 0) == iota((srows, srows), 1)
-    req_row = row_sum(eye, jnp.broadcast_to(req_col, eye.shape))
+    req_row = row_sum(eye, jnp.broadcast_to(by_slot, eye.shape))
     r_t = iota((rows, srows), 0)
     c_t = iota((rows, srows), 1)
-    back = (lax.div(r_t, batch) == lax.rem(c_t, HEADS)) & (lax.rem(r_t, batch) == req_row)
+    back = one_hot(
+        (lax.div(r_t, batch) == lax.rem(c_t, HEADS)) & (lax.rem(r_t, batch) == req_row)
+    )
+    live = jnp.concatenate(
+        [pos[j:j + 1, :] < len_col[j * HEADS:(j + 1) * HEADS] for j in range(slots)], axis=0
+    )
+    dead[...] = jnp.where(live, 0.0, -jnp.inf)
+    for c in slab_copies:
+        c.wait()
+    local[12].wait()
 
     def wait_q(k, carry):
         for c in q_copies(k):
@@ -196,48 +207,37 @@
     lax.fori_loop(1, n, wait_q, 0, unroll=unroll)
     qn = qn_all[...].astype(f32).reshape(rows, qn_all.shape[2]).astype(bf16)
     qr = qr_all[...].astype(f32).reshape(rows, qr_all.shape[2]).astype(bf16)
-    qn_hb = dot(one_hot(perm), qn)
-    for h in range(0, HEADS, 2):
-        two = [
-            dot(qn_hb[g * batch:(g + 1) * batch].astype(bf16), uk0[g]) for g in (h, h + 1)
-        ]
-        qlat[h * batch:(h + 2) * batch, :] = jnp.concatenate(two, axis=0).astype(bf16)
-    q_slot = dot(sel_hb, qlat[...]).astype(bf16)
-    r_slot = dot(sel_bh, qr).astype(bf16)
-
-    maxes, sums = [], []
+    qn_head = dot(sel_head, qn)
+    for h in range(HEADS):
+        at = slice(h * slots, (h + 1) * slots)
+        full = dot(qn_head[at].astype(bf16), uk0[h])
+        for t in range(qlat.shape[0]):
+            qlat[t, at, :] = full[:, t * lanes:(t + 1) * lanes]
+    r_slot = dot(sel_hot, qr).astype(bf16)
+
     for j in range(slots):
         at = slice(j * HEADS, (j + 1) * HEADS)
-        slab_copies[j].wait()
-        score = (
-            dot(q_slot[at], keys[j, :LATENT]) + dot(r_slot[at], keys[j, LATENT:])
-        ) * score_scale
-        live = pos[j:j + 1, :] < len_col[at]
-        block_max = jnp.max(jnp.where(live, score, neg_fill), axis=1, keepdims=True)
-        weight = jnp.where(
-            live, jnp.exp(jnp.where(live, score - block_max, 0.0)), 0.0
+        q_slot = jnp.concatenate(
+            [qlat[t, pl.ds(j, HEADS, stride=slots), :] for t in range(qlat.shape[0])], axis=1
         ).astype(bf16)
-        maxes.append(block_max)
-        sums.append(jnp.sum(weight.astype(f32), axis=1, keepdims=True))
-        slot_out[at, :] = dot_t(weight, keys[j, :LATENT])
-    slot_max = jnp.concatenate(maxes, axis=0)
-    slot_sum = jnp.concatenate(sums, axis=0)
-
-    max_row = row_sum(eye, jnp.broadcast_to(slot_max, eye.shape))
-    sum_row = row_sum(eye, jnp.broadcast_to(slot_sum, eye.shape))
-    dense_max = jnp.max(jnp.where(back, max_row, neg_fill), axis=1, keepdims=True)
-    factor_row = jnp.exp(max_row - row_sum(back, jnp.broadcast_to(dense_max, back.shape)))
-    dense_sum = lane_sum(back, jnp.broadcast_to(sum_row * factor_row, back.shape))
-    factor_col = lane_sum(eye, jnp.broadcast_to(factor_row, eye.shape))
-    scaled = (slot_out[...] * factor_col).astype(bf16)
-    dense = dot(one_hot(back), scaled)
-    local[12].wait()
+        score[at, :] = dot(q_slot, keys[j, :LATENT]) + dot(r_slot[at], keys[j, LATENT:])
+    masked = score[...] * score_scale + dead[...]
+    slot_max = jnp.max(masked, axis=1, keepdims=True)
+    stat_max = jnp.max(jnp.where(sel, slot_max, neg_fill), axis=0, keepdims=True)
+    group_max = jnp.max(jnp.where(sel, stat_max, neg_fill), axis=1, keepdims=True)
+    weight = jnp.exp(masked - group_max).astype(bf16)
+    slot_sum = jnp.sum(weight.astype(f32), axis=1, keepdims=True)
+    stat_sum = row_sum(sel, jnp.broadcast_to(slot_sum, sel.shape))
+    parts = [
+        dot_t(weight[j * HEADS:(j + 1) * HEADS], keys[j, :LATENT]).astype(bf16)
+        for j in range(slots)
+    ]
+
+    dense = dot(back, jnp.concatenate(parts, axis=0))
     for h in range(HEADS):
         part = dot(dense[h * batch:(h + 1) * batch].astype(bf16), uv0[h])
         proj[pl.ds(h, batch, stride=HEADS), :] = part
     outbox[:, :rows_dev, :] = proj[...].reshape(n, rows_dev, proj.shape[1])
-    stat_max = row_sum(perm, jnp.broadcast_to(dense_max, perm.shape))
-    stat_sum = row_sum(perm, jnp.broadcast_to(dense_sum, perm.shape))
     stats = jnp.concatenate([stat_max, stat_sum], axis=0)
     outbox[:, rows_dev:, :] = jnp.broadcast_to(stats[None], (n,) + stats.shape)
     inbox[me] = outbox[me]
@@ -332,8 +332,9 @@
             pltpu.VMEM(slab_map.shape, jnp.int32),
             pltpu.VMEM((width, deep_tok), bf16),
             pltpu.VMEM((batch, deep_tok), jnp.int32),
-            pltpu.VMEM((n * rows_dev, LATENT), bf16),
-            pltpu.VMEM((slots * HEADS, LATENT), f32),
+            pltpu.VMEM((LATENT // 128, slots * HEADS, 128), f32),
+            pltpu.VMEM((slots * HEADS, slab), f32),
+            pltpu.VMEM((slots * HEADS, slab), f32),
             pltpu.VMEM((n * rows_dev, value), f32),
             pltpu.VMEM((n, rows_dev + 2, value), f32),
             pltpu.VMEM((n, rows_dev + 2, value), f32),

time: 23.5 us -> 21.5 us (0.915)
  Pallas kernels: 22 us -> 20 us
    pallas_call x1, Pallas kernels: 22 us -> 20 us  [shards(): pl.pallas_call(functools.partial(kernel, n, (rows_dev, slots, batch)), ou...]
where the time goes in v3:
time: 21.5 us; the launch traced here: 21.3 us
  Pallas kernels  20 us (93%)
  local copies, waits for them, and re-layouts  1.28 us (6%)
    pallas_call x1, Pallas kernels, shards(): pl.pallas_call(functools.partial(kernel, n, (rows_dev, slots, batch)), ou...  20 us
    unnamed x1, local copies, waits for them, and re-layouts  1.28 us

profile of v3, /device:TPU:0, one launch (start us, length us, event | category | flops | bytes accessed | tf_op | source)
XLA Modules:
  0.0 21.3 jit_solution(4675493199087375660)
XLA Ops:
  0.0 20.0 %shard_map.109 = bf16[2,8,128]{2,1,0:T(8,128)(2,1)} custom-call(s32[8]{0:T(128)} %lengths.1, bf16[2,8,128]{2,1,0:T(8,128)(2,1)} %q_nope.1, bf16[2,8,64]{2,1,0:T(8,128)(2,1)} %q_rope.1, bf16[2,16,128,512]{3,2,1,0:T(8,128)(2,1)} %w_uk.1, bf16[2,16,512,128]{3,2,1,0:T(8,128)(2,1)} %w_uv.1, bf16[2,8,576]{2,1,0:T(8,128)(2,1)} %new_latent.1, ...), custom_call_target="tpu_custom_call" | custom-call | tf_op jit(solution)/shard_map/pallas_call | solution.py:315
  20.0 1.3 %copy.13 = bf16[2,8,128]{2,1,0:T(8,128)(2,1)} copy(bf16[2,8,128]{2,1,0:T(8,128)(2,1)} %shard_map.109) | data formatting | bytes 8192

commit v4 on v3

--- a/solution.py
+++ b/solution.py
@@ -48,8 +48,8 @@
     deep_cache, deep_positions,
     out,
     qn_all, qr_all, qn_deep, qr_deep, uk0, uv0, uk1, uv1, newlat, keys, pos, smap,
-    dkeys, dpos, qlat, score, dead, proj, outbox, inbox,
-    loc_sem, slab_sem, qn_send, qn_recv, qr_send, qr_recv, o_send, o_recv,
+    dkeys, dpos, qlat, score, dead, proj, outbox, inbox, stats,
+    loc_sem, slab_sem, qn_send, qn_recv, qr_send, qr_recv, o_send, o_recv, st_send, st_recv,
 ):
     rows_dev, slots, batch = dims
     rows = n * rows_dev
@@ -60,6 +60,14 @@
     req = lax.div(start, HEADS)
     pad = max(8, rows_dev)
     unroll = n <= 16
+
+    def spread(body):
+        if unroll:
+            for k in sorted(range(1, n), key=lambda k: -abs(k - n // 2)):
+                body(k, 0)
+        else:
+            lax.fori_loop(1, n, body, 0)
+
     lanes = qlat.shape[2]
 
     local = [
@@ -94,7 +102,7 @@
         )
         return carry
 
-    lax.fori_loop(1, n, greet, 0, unroll=unroll)
+    spread(greet)
     for c in local[2:12]:
         c.start()
     for c in slab_copies:
@@ -122,7 +130,7 @@
             c.start()
         return carry
 
-    lax.fori_loop(1, n, send_q, 0, unroll=unroll)
+    spread(send_q)
 
     def widen(x):
         if x.shape[0] < pad:
@@ -237,19 +245,22 @@
     for h in range(HEADS):
         part = dot(dense[h * batch:(h + 1) * batch].astype(bf16), uv0[h])
         proj[pl.ds(h, batch, stride=HEADS), :] = part
-    outbox[:, :rows_dev, :] = proj[...].reshape(n, rows_dev, proj.shape[1])
-    stats = jnp.concatenate([stat_max, stat_sum], axis=0)
-    outbox[:, rows_dev:, :] = jnp.broadcast_to(stats[None], (n,) + stats.shape)
+    outbox[...] = proj[...].reshape(outbox.shape).astype(bf16)
+    stats[me] = jnp.concatenate([stat_max, stat_sum], axis=0)
     inbox[me] = outbox[me]
 
-    def o_copy(k):
-        return remote(outbox.at[lax.rem(me + k, n)], inbox.at[me], o_send, o_recv, k)
+    def o_copies(k):
+        return (
+            remote(outbox.at[lax.rem(me + k, n)], inbox.at[me], o_send, o_recv, k),
+            remote(stats.at[me], stats.at[me], st_send, st_recv, k),
+        )
 
     def send_o(k, carry):
-        o_copy(k).start()
-        return carry
-
-    lax.fori_loop(1, n, send_o, 0, unroll=unroll)
+        for c in o_copies(k):
+            c.start()
+        return carry
+
+    spread(send_o)
 
     qn0 = widen(qn_all[me].astype(f32)).astype(bf16)
     qr0 = widen(qr_all[me].astype(f32)).astype(bf16)
@@ -266,12 +277,13 @@
     lax.fori_loop(1, n, wait_sent, 0, unroll=unroll)
 
     def wait_o(k, carry):
-        o_copy(k).wait_recv()
+        for c in o_copies(k):
+            c.wait_recv()
         return carry
 
     lax.fori_loop(1, n, wait_o, 0, unroll=unroll)
-    got_max = inbox[:, rows_dev, :]
-    got_sum = inbox[:, rows_dev + 1, :]
+    got_max = stats[:, 0, :]
+    got_sum = stats[:, 1, :]
     far_max = jnp.max(got_max, axis=0, keepdims=True)
     got_f = jnp.exp(got_max - far_max)
     far_sum = jnp.sum(got_sum * got_f, axis=0, keepdims=True)
@@ -282,7 +294,7 @@
 
     acc = jnp.zeros((rows_dev, proj.shape[1]), f32)
     for s in range(n):
-        acc = acc + own_rows(got_f[s:s + 1]) * inbox[s, :rows_dev, :]
+        acc = acc + own_rows(got_f[s:s + 1]) * inbox[s].astype(f32)
     far_max = own_rows(far_max)
     far_sum = own_rows(far_sum)
     own_score = own_score[:rows_dev]
@@ -293,7 +305,8 @@
     out[0] = ((own_f * new_out[:rows_dev] + acc * far_f) / total).astype(bf16)
 
     def wait_o_sent(k, carry):
-        o_copy(k).wait_send()
+        for c in o_copies(k):
+            c.wait_send()
         return carry
 
     lax.fori_loop(1, n, wait_o_sent, 0, unroll=unroll)
@@ -336,10 +349,13 @@
             pltpu.VMEM((slots * HEADS, slab), f32),
             pltpu.VMEM((slots * HEADS, slab), f32),
             pltpu.VMEM((n * rows_dev, value), f32),
-            pltpu.VMEM((n, rows_dev + 2, value), f32),
-            pltpu.VMEM((n, rows_dev + 2, value), f32),
+            pltpu.VMEM((n, rows_dev, value), bf16),
+            pltpu.VMEM((n, rows_dev, value), bf16),
+            pltpu.VMEM((n, 2, n * rows_dev), f32),
             dma((13,)),
             dma((slots,)),
+            dma((n,)),
+            dma((n,)),
             dma((n,)),
             dma((n,)),
             dma((n,)),

time: 21.5 us -> 21.4 us (level)
  no operation moved by 1% of the time
where the time goes in v4:
time: 21.4 us; the launch traced here: 21.2 us
  Pallas kernels  19.9 us (93%)
  local copies, waits for them, and re-layouts  1.28 us (6%)
    pallas_call x1, Pallas kernels, shards(): pl.pallas_call(functools.partial(kernel, n, (rows_dev, slots, batch)), ou...  19.9 us
    unnamed x1, local copies, waits for them, and re-layouts  1.28 us

profile of v4, /device:TPU:0, one launch (start us, length us, event | category | flops | bytes accessed | tf_op | source)
XLA Modules:
  0.0 21.2 jit_solution(17972945782175916319)
XLA Ops:
  0.0 19.9 %shard_map.109 = bf16[2,8,128]{2,1,0:T(8,128)(2,1)} custom-call(s32[8]{0:T(128)} %lengths.1, bf16[2,8,128]{2,1,0:T(8,128)(2,1)} %q_nope.1, bf16[2,8,64]{2,1,0:T(8,128)(2,1)} %q_rope.1, bf16[2,16,128,512]{3,2,1,0:T(8,128)(2,1)} %w_uk.1, bf16[2,16,512,128]{3,2,1,0:T(8,128)(2,1)} %w_uv.1, bf16[2,8,576]{2,1,0:T(8,128)(2,1)} %new_latent.1, ...), custom_call_target="tpu_custom_call" | custom-call | tf_op jit(solution)/shard_map/pallas_call | solution.py:328
  19.9 1.3 %copy.13 = bf16[2,8,128]{2,1,0:T(8,128)(2,1)} copy(bf16[2,8,128]{2,1,0:T(8,128)(2,1)} %shard_map.109) | data formatting | bytes 8192
